TPU v7x, 32 devices: a whole 2x2x4 slice. The times are simulated.
32 devices in a mesh: gx: 16 (over z, y, x), gy: 2 (over core).
Axes of the slice: x: 2, y: 2, z: 4, core: 2. Of those that a mesh axis runs over, the one named last changes fastest.
Arguments:
- operator: float32 [243, 32768], P(None, ('gx', 'gy')), may hold values from -0.6 to 10.6
- basis_u: float32 [144, 32768], P(None, ('gx', 'gy')), may hold values from -6 to 6
- basis_c: float32 [144, 32768], P(None, ('gx', 'gy')), may hold values from -6 to 6
- right_side: float32 [3, 32768], P(None, ('gx', 'gy')), may hold values from -16 to 16
- new_rows: int32 [32768], P(('gx', 'gy')), may hold values from 0 to 32767, as said below
Outputs:
- solution: float32 [3, 32768], P(None, ('gx', 'gy'))
- residual: float32 [3, 32768], P(None, ('gx', 'gy'))
Inputs may be any that keep to these rules, and one draw needn't show every extreme that they name: `new_rows`: each block row gets one new index (a permutation). Each device sends 0 to 64 of its old rows to each device, and each device both sends exactly 64 rows to some peer and receives exactly 64 rows from some peer.
All inputs are finite; a program needn't handle non-finite values.
Results may differ from a plain program's by a relative error of at most 0.0003.
Values sent between devices are 32-bit elements; how exact they have to be, the bound alone decides.
A program may use at most 64 MiB of HBM per device.

v0:
```python
import jax
import jax.numpy as jnp
from jax import lax
from jax.sharding import PartitionSpec as P

CX = 1
CY = 8
CZ = 128
K = 48


def with_halo(cells, sides, width):
    for axis, dim in sides:
        count = lax.axis_size(axis)
        ends = count - 1
        head = lax.slice_in_dim(cells, 0, width, axis=dim)
        tail = lax.slice_in_dim(cells, cells.shape[dim] - width, cells.shape[dim], axis=dim)
        cells = jnp.concatenate(
            [
                lax.ppermute(tail, axis, [(i, (i + 1) % count) for i in range(ends)]),
                cells,
                lax.ppermute(head, axis, [((i + 1) % count, i) for i in range(ends)]),
            ],
            axis=dim,
        )
    return cells


def stencil(coef, padded):
    size_x = padded.shape[1] - 2
    size_y = padded.shape[2] - 2
    size_z = padded.shape[3] - 2
    total = jnp.zeros((3, size_x, size_y, size_z), jnp.float32)
    for k in range(27):
        dx, dy, dz = (k // 9, k // 3 % 3, k % 3)
        moved = padded[:, dx : dx + size_x, dy : dy + size_y, dz : dz + size_z]
        total = total + jnp.sum(coef[k] * moved[None], axis=1)
    return total


def apply_op(coef, vector):
    block = vector.reshape(3, CX, CY, CZ)
    padded = with_halo(block, (("gx", 1), ("gy", 2)), 1)
    padded = jnp.pad(padded, ((0, 0), (0, 0), (0, 0), (1, 1)))
    return stencil(coef, padded).reshape(3, CX * CY * CZ)


def project(basis, vector):
    return jnp.einsum("amp,ap->m", basis, vector, precision=lax.Precision.HIGHEST)


def combine(basis, coeffs):
    return jnp.einsum("amp,m->ap", basis, coeffs, precision=lax.Precision.HIGHEST)


def body(operator, basis_u, basis_c, right_side, new_rows):
    rows = operator.shape[1]
    count_x = lax.axis_size("gx")
    count_y = lax.axis_size("gy")
    peers = count_x * count_y
    capacity = 2 * rows // peers
    payload = jnp.concatenate([operator, basis_u, basis_c, right_side], 0)
    c_start = 243 + 3 * K
    width = payload.shape[0]
    target = new_rows // rows
    local_row = new_rows % rows
    onehot = (target[:, None] == jnp.arange(peers, dtype=jnp.int32)[None, :]).astype(jnp.int32)
    rank = jnp.sum(jnp.cumsum(onehot, 0) * onehot, 1) - 1
    slot = target * capacity + rank
    buffer = jnp.zeros((width, peers * capacity), jnp.float32).at[:, slot].set(payload)
    labels = jnp.full((1, peers * capacity), rows, jnp.int32).at[0, slot].set(local_row)
    got, tags = (
        lax.all_to_all(buffer, ("gx", "gy"), split_axis=1, concat_axis=1, tiled=True),
        lax.all_to_all(labels, ("gx", "gy"), split_axis=1, concat_axis=1, tiled=True),
    )
    placed = jnp.zeros((width, rows), jnp.float32).at[:, tags[0]].set(got, mode="drop")
    coef = placed[:243].reshape(27, 3, 3, CX, CY, CZ)
    c_rows = placed[c_start : c_start + 3 * K].reshape(3, K, rows)
    load = placed[c_start + 3 * K :]
    gram_local = jnp.einsum("amp,anp->mn", c_rows, c_rows, precision=lax.Precision.HIGHEST)
    eye = jnp.eye(K, dtype=jnp.float32)
    gram, raw_start, load_sq = lax.psum(
        (
            gram_local,
            jnp.einsum("amp,ap->m", c_rows, load, precision=lax.Precision.HIGHEST),
            jnp.sum(load * load),
        ),
        ("gx", "gy"),
    )
    lower_inv = jax.scipy.linalg.solve_triangular(jnp.linalg.cholesky(gram), eye, lower=True)
    cq = jnp.einsum("mn,anp->amp", lower_inv, c_rows, precision=lax.Precision.HIGHEST)
    start = jnp.dot(lower_inv, raw_start, precision=lax.Precision.HIGHEST)
    first_r = load - combine(cq, start)
    beta = jnp.sqrt(load_sq - jnp.sum(start * start))
    vec_one = first_r / beta

    def sums_of(image, vectors):
        local = (
            (project(cq, image),)
            + tuple((jnp.sum(vector * image) for vector in vectors))
            + (jnp.sum(image * image),)
        )
        return lax.psum(local, ("gx", "gy"))

    image = apply_op(coef, vec_one)
    proj_one, h11, image_sq = sums_of(image, (vec_one,))
    h21 = jnp.sqrt(image_sq - jnp.sum(proj_one * proj_one) - h11 * h11)
    vec_two = (image - combine(cq, proj_one) - h11 * vec_one) / h21
    image = apply_op(coef, vec_two)
    proj_two, h12, h22, image_sq = sums_of(image, (vec_one, vec_two))
    h32 = jnp.sqrt(image_sq - jnp.sum(proj_two * proj_two) - h12 * h12 - h22 * h22)
    m11 = h11 * h11 + h21 * h21
    m12 = h11 * h12 + h21 * h22
    m22 = h12 * h12 + h22 * h22 + h32 * h32
    g_one = beta * h11
    g_two = beta * h12
    determ = m11 * m22 - m12 * m12
    y_one = (m22 * g_one - m12 * g_two) / determ
    y_two = (m11 * g_two - m12 * g_one) / determ
    mixing = start - y_one * proj_one - y_two * proj_two
    u_weights = jnp.dot(lower_inv.T, mixing, precision=lax.Precision.HIGHEST)
    u_rows = placed[243 : 243 + 3 * K].reshape(3, K, rows)
    u_term = combine(u_rows, u_weights)
    solution = u_term + y_one * vec_one + y_two * vec_two
    residual = load - apply_op(coef, solution)
    return (solution, residual)


def solution(mesh):
    placed = (
        P(None, ("gx", "gy")),
        P(None, ("gx", "gy")),
        P(None, ("gx", "gy")),
        P(None, ("gx", "gy")),
        P(("gx", "gy")),
    )
    return jax.shard_map(
        body,
        mesh=mesh,
        in_specs=placed,
        out_specs=(P(None, ("gx", "gy")), P(None, ("gx", "gy"))),
        check_vma=False,
    )
```

profile of v0, /device:TPU:0, one launch (start us, length us, event | category | flops | bytes accessed | tf_op | source)
XLA Modules:
  0.0 611.0 jit_solution(12784851384346756027)
XLA Ops:
  1.3 9.0 %reduce-window.6 = s32[32,8,128]{2,1,0:T(8,128)S(1)} reduce-window(s32[32,8,128]{2,1,0:T(8,128)S(1)} %fusion.11, s32[]{:T(128)} %constant.82.clone.1), window={size=1x1x128 pad=0_0x0_0x127_0}, to_apply=%region_0.1 | reduce-window | flops 4161536 | bytes 262148 | tf_op jit(solution)/shard_map/reduce-window
  12.4 4.3 scatter_custom_fusion.2
  17.4 7.3 %all-to-all-start = ((s32[1,32,64]{2,0,1:T(1,128)}), s32[1,32,64]{2,0,1:T(1,128)S(1)}, u32[]{:S(2)}, u32[]{:S(2)}) async-start(s32[1,32,64]{2,0,1:T(1,128)} %all_to_all.14), calls=%async_computation | async-start | bytes 32768 | tf_op jit(solution)/shard_map/all_to_all | solution.py:74
  26.5 2.1 copy.234
  28.6 8.2 %scatter_custom_fusion = f32[534,2048]{0,1:T(8,128)} fusion(s32[1024]{0:T(1024)S(1)} %compare_select_fusion.1, f32[1024,534]{1,0:T(8,128)} %copy.234, f32[]{:T(128)} %constant.79.clone.1), kind=kCustom, calls=%fused_computation.3 | custom fusion | bytes 4375040 | tf_op jit(solution)/shard_map/scatter | solution.py:70
  36.8 5.9 all-to-all-start.1
  44.0 115.2 %all-to-all-done.1 = f32[534,32,64]{0,2,1:T(8,128)} async-done(((f32[534,32,64]{0,2,1:T(8,128)}), f32[534,32,64]{0,2,1:T(8,128)}, u32[]{:S(2)}, u32[]{:S(2)}) %all-to-all-start.1) | async-done | bytes 4374560 | tf_op jit(solution)/shard_map/all_to_all | solution.py:73
  159.2 10.4 %scatter_custom_fusion.1 = f32[534,1024]{0,1:T(8,128)S(1)} fusion(s32[2048]{0:T(1024)S(1)} %bitcast.705, f32[2048,534]{1,0:T(8,128)} %bitcast.8, f32[]{:T(128)} %constant.79.clone.1), kind=kCustom, calls=%fused_computation.6 | custom fusion | bytes 2187776 | tf_op jit(solution)/shard_map/scatter | solution.py:76
  170.4 2.0 fusion.40
  175.3 38.6 %all-reduce.6 = (f32[48,48]{0,1:T(8,128)S(1)}, f32[48]{0:T(128)S(1)}, f32[]{:T(128)}) all-reduce(f32[48,48]{0,1:T(8,128)S(1)} %convolution_bitcast_fusion.1, f32[48]{0:T(128)S(1)} %convolution_bitcast_fusion.5, f32[]{:T(128)} %get-tuple-element.56), channel_id=1, replica_groups=mesh['gx'=16,'gy'=2] {'gx','gy'}, use_global_device_ids=true, to_apply=%region_6.7 | all-reduce | flops 2353 | bytes 18824 | tf_op jit(solution)/shard_map/psum | solution.py:82
  214.0 4.4 cholesky.17
  219.7 3.7 custom-call.7
  233.0 5.4 collective-permute-start
  238.4 2.9 fusion.39
  241.4 6.4 %fusion.38 = (f32[9,1024]{0,1:T(8,128)}, f32[9,1024]{0,1:T(8,128)}, f32[9,1024]{0,1:T(8,128)}, f32[9,1024]{0,1:T(8,128)}, f32[9,1024]{0,1:T(8,128)}, /*index=5*/...) fusion(f32[534,1024]{0,1:T(8,128)S(1)} %scatter_custom_fusion.1), kind=kLoop, calls=%fused_computation.249 | loop fusion | bytes 1400832 | tf_op jit(solution)/shard_map/slice | solution.py:37
  250.5 2.4 copy.235
  274.9 1.9 copy.267
  277.6 1.9 copy.265
  280.9 1.8 copy.263
  284.3 1.8 copy.261
  287.6 1.8 copy.259
  290.9 1.8 copy.258
  294.2 1.8 copy.257
  297.5 1.8 copy.254
  300.9 1.8 copy.253
  304.2 1.8 copy.252
  307.5 1.8 copy.251
  312.2 1.9 collective-permute-start.2
  353.1 2.1 multiply_reduce_fusion.86
  356.9 4.3 multiply_reduce_fusion.2
  361.2 1.8 copy.316
  363.0 2.2 convolution_bitcast_fusion.4
  365.2 42.6 %all-reduce.5 = (f32[48]{0:T(128)}, f32[]{:T(128)}, f32[]{:T(128)}) all-reduce(f32[48]{0:T(128)} %convolution_bitcast_fusion.4, f32[]{:T(128)} %get-tuple-element.27, f32[]{:T(128)} %get-tuple-element.25), channel_id=1, replica_groups=mesh['gx'=16,'gy'=2] {'gx','gy'}, use_global_device_ids=true, to_apply=%region_40.41 | all-reduce | flops 50 | bytes 400 | tf_op jit(solution)/shard_map/psum | solution.py:103
  409.0 2.1 fusion.27
  415.2 2.6 fusion.7
  424.7 5.4 collective-permute-start.4
  435.5 4.2 collective-permute-start.6
  484.7 2.1 multiply_reduce_fusion.85
  488.5 4.5 multiply_reduce_fusion
  494.9 2.2 convolution_bitcast_fusion.3
  497.1 43.6 %all-reduce.4 = (f32[48]{0:T(128)}, f32[]{:T(128)}, f32[]{:T(128)}, f32[]{:T(128)}) all-reduce(f32[48]{0:T(128)} %convolution_bitcast_fusion.3, f32[]{:T(128)} %get-tuple-element.11, f32[]{:T(128)} %get-tuple-element.10, f32[]{:T(128)} %get-tuple-element.22), channel_id=1, replica_groups=mesh['gx'=16,'gy'=2] {'gx','gy'}, use_global_device_ids=true, to_apply=%region_79.80 | all-reduce | flops 51 | bytes 408 | tf_op jit(solution)/shard_map/psum | solution.py:103
  549.2 2.1 fusion.44
  553.0 2.1 fusion.5
  555.1 1.8 copy.311
  559.4 4.8 collective-permute-start.8
  571.5 4.2 collective-permute-start.10
  605.6 3.6 fusion.4
  609.1 1.8 copy.312
  (270 shorter events, 208.6 us)
Async XLA Ops:
  17.4 19.4 %all-to-all-start = ((s32[1,32,64]{2,0,1:T(1,128)}), s32[1,32,64]{2,0,1:T(1,128)S(1)}, u32[]{:S(2)}, u32[]{:S(2)}) async-start(s32[1,32,64]{2,0,1:T(1,128)} %all_to_all.14), calls=%async_computation | async-start | bytes 32768 | tf_op jit(solution)/shard_map/all_to_all | solution.py:74
  36.8 122.4 %all-to-all-start.1 = ((f32[534,32,64]{0,2,1:T(8,128)}), f32[534,32,64]{0,2,1:T(8,128)}, u32[]{:S(2)}, u32[]{:S(2)}) async-start(f32[534,32,64]{0,2,1:T(8,128)} %bitcast.480), calls=%async_computation.1 | async-start | bytes 10485760 | tf_op jit(solution)/shard_map/all_to_all | solution.py:73
  223.6 1.5 copy-start.1
  231.7 79.1 %collective-permute-start.1 = (f32[3,1,8,128]{3,1,2,0:T(1,128)}, f32[3,1,8,128]{3,1,2,0:T(1,128)}, u32[]{:S(2)}, u32[]{:S(2)}) collective-permute-start(f32[3,1,8,128]{3,1,2,0:T(1,128)} %copy.240), channel_id=1, source_target_pairs={{2,0},{4,2},{6,4},{8,6},{10,8},{12,10},{14,12},{16,14},{18,16},{20... | collective-permute-start | bytes 36872 | tf_op jit(solution)/shard_map/ppermute | solution.py:22
  233.0 77.8 %collective-permute-start = (f32[3,1,8,128]{3,1,2,0:T(1,128)}, f32[3,1,8,128]{3,1,2,0:T(1,128)}, u32[]{:S(2)}, u32[]{:S(2)}) collective-permute-start(f32[3,1,8,128]{3,1,2,0:T(1,128)} %copy.240), channel_id=1, source_target_pairs={{0,2},{2,4},{4,6},{6,8},{8,10},{10,12},{12,14},{14,16},{16,18},{18... | collective-permute-start | bytes 36872 | tf_op jit(solution)/shard_map/ppermute | solution.py:20
  249.3 0.6 copy-start
  312.2 7.9 %collective-permute-start.2 = (f32[3,3,1,128]{3,1,2,0:T(4,128)}, f32[3,3,1,128]{3,1,2,0:T(4,128)}, u32[]{:S(2)}, u32[]{:S(2)}) collective-permute-start(f32[3,3,1,128]{3,1,2,0:T(4,128)} %get-tuple-element.136), channel_id=1, source_target_pairs={{0,1},{2,3},{4,5},{6,7},{8,9},{10,11},{12,13},{14,15},{16,17},{18,... | collective-permute-start | bytes 13832 | tf_op jit(solution)/shard_map/ppermute | solution.py:20
  314.0 6.0 collective-permute-start.3
  421.5 8.6 %collective-permute-start.5 = (f32[3,1,8,128]{3,1,2,0:T(1,128)}, f32[3,1,8,128]{3,1,2,0:T(1,128)}, u32[]{:S(2)}, u32[]{:S(2)}) collective-permute-start(f32[3,1,8,128]{3,1,2,0:T(1,128)} %copy.281), channel_id=1, source_target_pairs={{2,0},{4,2},{6,4},{8,6},{10,8},{12,10},{14,12},{16,14},{18,16},{20... | collective-permute-start | bytes 36872 | tf_op jit(solution)/shard_map/ppermute | solution.py:22
  424.7 6.8 %collective-permute-start.4 = (f32[3,1,8,128]{3,1,2,0:T(1,128)}, f32[3,1,8,128]{3,1,2,0:T(1,128)}, u32[]{:S(2)}, u32[]{:S(2)}) collective-permute-start(f32[3,1,8,128]{3,1,2,0:T(1,128)} %copy.281), channel_id=1, source_target_pairs={{0,2},{2,4},{4,6},{6,8},{8,10},{10,12},{12,14},{14,16},{16,18},{18... | collective-permute-start | bytes 36872 | tf_op jit(solution)/shard_map/ppermute | solution.py:20
  432.8 8.6 %collective-permute-start.7 = (f32[3,3,1,128]{3,1,2,0:T(4,128)}, f32[3,3,1,128]{3,1,2,0:T(4,128)}, u32[]{:S(2)}, u32[]{:S(2)}) collective-permute-start(f32[3,3,1,128]{3,1,2,0:T(4,128)} %get-tuple-element.135), channel_id=1, source_target_pairs={{1,0},{3,2},{5,4},{7,6},{9,8},{11,10},{13,12},{15,14},{17,16},{19,... | collective-permute-start | bytes 13832 | tf_op jit(solution)/shard_map/ppermute | solution.py:22
  435.5 11.0 %collective-permute-start.6 = (f32[3,3,1,128]{3,1,2,0:T(4,128)}, f32[3,3,1,128]{3,1,2,0:T(4,128)}, u32[]{:S(2)}, u32[]{:S(2)}) collective-permute-start(f32[3,3,1,128]{3,1,2,0:T(4,128)} %get-tuple-element.134), channel_id=1, source_target_pairs={{0,1},{2,3},{4,5},{6,7},{8,9},{10,11},{12,13},{14,15},{16,17},{18,... | collective-permute-start | bytes 13832 | tf_op jit(solution)/shard_map/ppermute | solution.py:20
  558.1 13.4 %copy-start.4 = (f32[3,1,8,128]{3,1,2,0:T(1,128)}, f32[3,1,8,128]{3,1,2,0:T(1,128)S(1)}, u32[]{:S(2)}) copy-start(f32[3,1,8,128]{3,1,2,0:T(1,128)S(1)} %copy.296) | copy-start | bytes 36868
  558.1 8.7 %collective-permute-start.9 = (f32[3,1,8,128]{3,1,2,0:T(1,128)S(1)}, f32[3,1,8,128]{3,1,2,0:T(1,128)S(1)}, u32[]{:S(2)}, u32[]{:S(2)}) collective-permute-start(f32[3,1,8,128]{3,1,2,0:T(1,128)S(1)} %copy.296), channel_id=1, source_target_pairs={{2,0},{4,2},{6,4},{8,6},{10,8},{12,10},{14,12},{16,14},{18,16},{20... | collective-permute-start | bytes 36872 | tf_op jit(solution)/shard_map/ppermute | solution.py:22
  559.4 8.8 %collective-permute-start.8 = (f32[3,1,8,128]{3,1,2,0:T(1,128)S(1)}, f32[3,1,8,128]{3,1,2,0:T(1,128)S(1)}, u32[]{:S(2)}, u32[]{:S(2)}) collective-permute-start(f32[3,1,8,128]{3,1,2,0:T(1,128)S(1)} %copy.296), channel_id=1, source_target_pairs={{0,2},{2,4},{4,6},{6,8},{8,10},{10,12},{12,14},{14,16},{16,18},{18... | collective-permute-start | bytes 36872 | tf_op jit(solution)/shard_map/ppermute | solution.py:20
  566.9 4.7 copy-start.2
  568.2 3.3 copy-start.3
  568.9 7.8 %collective-permute-start.11 = (f32[3,3,1,128]{3,1,2,0:T(4,128)}, f32[3,3,1,128]{3,1,2,0:T(4,128)}, u32[]{:S(2)}, u32[]{:S(2)}) collective-permute-start(f32[3,3,1,128]{3,1,2,0:T(4,128)} %get-tuple-element.133), channel_id=1, source_target_pairs={{1,0},{3,2},{5,4},{7,6},{9,8},{11,10},{13,12},{15,14},{17,16},{19,... | collective-permute-start | bytes 13832 | tf_op jit(solution)/shard_map/ppermute | solution.py:22
  571.5 10.2 %collective-permute-start.10 = (f32[3,3,1,128]{3,1,2,0:T(4,128)}, f32[3,3,1,128]{3,1,2,0:T(4,128)}, u32[]{:S(2)}, u32[]{:S(2)}) collective-permute-start(f32[3,3,1,128]{3,1,2,0:T(4,128)} %get-tuple-element.132), channel_id=1, source_target_pairs={{0,1},{2,3},{4,5},{6,7},{8,9},{10,11},{12,13},{14,15},{16,17},{18,... | collective-permute-start | bytes 13832 | tf_op jit(solution)/shard_map/ppermute | solution.py:20
  588.7 13.7 %copy-start.7 = (f32[3,8,128]{2,1,0:T(8,128)S(1)}, f32[3,8,128]{2,1,0:T(8,128)}, u32[]{:S(2)}) copy-start(f32[3,8,128]{2,1,0:T(8,128)} %multiply_reduce_fusion.4) | copy-start | bytes 36868
  589.6 13.9 %copy-start.6 = (f32[3,8,128]{2,1,0:T(8,128)S(1)}, f32[3,8,128]{2,1,0:T(8,128)}, u32[]{:S(2)}) copy-start(f32[3,8,128]{2,1,0:T(8,128)} %multiply_reduce_fusion.11) | copy-start | bytes 36868
  594.3 10.2 %copy-start.5 = (f32[3,8,128]{2,1,0:T(8,128)S(1)}, f32[3,8,128]{2,1,0:T(8,128)}, u32[]{:S(2)}) copy-start(f32[3,8,128]{2,1,0:T(8,128)} %multiply_reduce_fusion.5) | copy-start | bytes 36868
where the time goes:
time: 619 us; the launch traced here: 611 us
  local copies, waits for them, and re-layouts  171 us (28%)
  other arithmetic  126 us (20%)
  blocking collectives  125 us (20%)
  waiting for transfers between devices  115 us (19%)
  starting transfers between devices  47 us (8%)
  matrix products  14.6 us (2%)
  between operations  12 us (2%)
    all_to_all x1, waiting for transfers between devices, body(): lax.all_to_all(buffer, ('gx', 'gy'), split_axis=1, concat_axis=1, tiled=T...  115 us
    psum x2, blocking collectives, sums_of(): return lax.psum(local, ('gx', 'gy'))  86.2 us
    reduce_sum x69, other arithmetic, stencil(): total = total + jnp.sum(coef[k] * moved[None], axis=1)  62.8 us
    slice x29, local copies, waits for them, and re-layouts, stencil(): total = total + jnp.sum(coef[k] * moved[None], axis=1)  49.3 us
    reduce_sum x30, local copies, waits for them, and re-layouts, stencil(): total = total + jnp.sum(coef[k] * moved[None], axis=1)  44.8 us
    psum x1, blocking collectives, body(): lax.psum((gram_local, jnp.einsum('amp,ap->m', c_rows, load, precision=lax...  38.6 us
    unnamed x73, local copies, waits for them, and re-layouts  27.6 us
    ppermute x6, starting transfers between devices, with_halo(): lax.ppermute(tail, axis, [(i, (i + 1) % count) for i in range(ends)])  25.9 us
  transfers between devices with their start and end apart: 14, of which 1 were waited for; matrix products, arithmetic and copies ran while one was open for 18% of the time, Pallas kernels for 0%

commit v1 on v0

v1 whole, which is shorter than its diff:
```python
import functools

import jax
import jax.numpy as jnp
from jax import lax
from jax.experimental import pallas as pl
from jax.experimental.pallas import tpu as pltpu
from jax.sharding import PartitionSpec as P

CY = 8
CZ = 128
F32 = jnp.float32
BF16 = jnp.bfloat16
HIGH = lax.Precision.HIGHEST
NT = (((1,), (1,)), ((), ()))


def round_up(n, m):
    return (n + m - 1) // m * m


class Plan:
    def __init__(self, nx, ny, rows, op_rows, basis_rows):
        self.nx, self.ny, self.rows = nx, ny, rows
        self.peers = nx * ny
        self.k = basis_rows // 3
        self.op_rows, self.basis_rows = op_rows, basis_rows
        self.cap = 2 * rows // self.peers
        self.fold = CZ // self.cap
        self.c0 = round_up(op_rows, 8)
        self.b0 = self.c0 + basis_rows
        self.tag = self.b0 + 3
        self.part = round_up(-(-(self.tag + 1) // self.fold), 8)
        self.width = round_up(self.part * self.fold, 16)
        self.part = self.width // self.fold
        self.nblk = 2 * rows // 256
        self.per_blk = 2 * self.fold
        self.tiles = (self.k + 2 + 7) // 8
        self.stride = max(1, self.peers // 8)


def kernel(
    pn, op_ref, u_ref, c_ref, b_ref, rcol_ref, rrow_ref, sol_ref, res_ref,
    pay, hl, slot, ohp, xs, snd, got, xhl, oht, acc, new, uv,
    gpart, grs, gsnd, gfull, gm, ginv,
    hsnd, hrcv, mred, rsnd, rrcv, ulhs, usnd, urcv,
    bulk_s, bulk_r, rs_s, rs_r, ag_s, ag_r, h_s, h_r, red_s, red_r, u_s, u_r,
):
    gx, gy = lax.axis_index("gx"), lax.axis_index("gy")
    me = gx * pn.ny + gy
    peers, rows, k = pn.peers, pn.rows, pn.k

    def dev(p):
        return {"gx": lax.div(p, pn.ny), "gy": lax.rem(p, pn.ny)}

    def remote(src, dst, ssem, rsem, p):
        return pltpu.make_async_remote_copy(
            src_ref=src, dst_ref=dst, send_sem=ssem, recv_sem=rsem,
            device_id=dev(p), device_id_type=pl.DeviceIdType.MESH,
        )

    def others(body):
        def step(d, _):
            body(lax.rem(me + d, peers))
            return 0
        lax.fori_loop(1, peers, step, 0)

    barrier = pltpu.get_barrier_semaphore()
    others(lambda p: pl.semaphore_signal(
        barrier, inc=1, device_id=dev(p), device_id_type=pl.DeviceIdType.MESH))

    pay[0 : pn.op_rows, :] = op_ref[...]
    pay[pn.op_rows : pn.c0, :] = jnp.zeros((pn.c0 - pn.op_rows, rows), F32)
    pay[pn.c0 : pn.b0, :] = c_ref[...]
    pay[pn.b0 : pn.width, :] = jnp.zeros((pn.width - pn.b0, rows), F32)
    pay[pn.b0 : pn.tag, :] = b_ref[...]
    shift = rows.bit_length() - 1
    local = lax.bitwise_and(rrow_ref[...], rows - 1) + 1
    pay[pn.tag : pn.tag + 1, :] = local.astype(F32)

    gpart[...] = jnp.zeros(gpart.shape, F32)
    gram = jnp.zeros((k, k), F32)
    raw = jnp.zeros((1, k), F32)
    b8 = pay[pn.b0 : pn.b0 + 8, :]
    for a in range(3):
        ca = pay[pn.c0 + a * k : pn.c0 + (a + 1) * k, :]
        gram = gram + lax.dot_general(ca, ca, NT, precision=HIGH, preferred_element_type=F32)
        raw = raw + lax.dot_general(b8, ca, NT, precision=HIGH, preferred_element_type=F32)[a : a + 1]
    b3 = pay[pn.b0 : pn.tag, :]
    bb = jnp.sum(jnp.sum(b3 * b3, axis=1, keepdims=True), axis=0, keepdims=True)
    gpart[0:k, 0:k] = gram
    gpart[k : k + 1, 0:k] = raw
    gpart[k + 1 : k + 2, :] = jnp.broadcast_to(bb, (1, CZ))

    pl.semaphore_wait(barrier, peers - 1)

    def tile(t):
        return pl.ds(pl.multiple_of(t * 8, 8), 8)

    def rs_send(t, _):
        own = t * pn.stride

        @pl.when(me != own)
        def _():
            remote(gpart.at[tile(t), :], grs.at[me], rs_s.at[t], rs_r.at[me], own).start()
        return 0

    lax.fori_loop(0, pn.tiles, rs_send, 0)

    trow = lax.shift_right_logical(rrow_ref[...], shift)
    jrow = lax.broadcasted_iota(jnp.int32, (CZ, rows), 1)
    irow = lax.broadcasted_iota(jnp.int32, (CZ, rows), 0)

    def slots(i, _):
        at = pl.ds(pl.multiple_of(i * CZ, CZ), CZ)
        tc = lax.shift_right_logical(rcol_ref[at, :], shift)
        before = jnp.logical_and(tc == trow, jrow < irow + i * CZ)
        rank = jnp.sum(jnp.where(before, 1.0, 0.0), axis=1, keepdims=True)
        slot[at, :] = jnp.broadcast_to(tc * pn.cap + rank.astype(jnp.int32), (CZ, CZ))
        return 0

    lax.fori_loop(0, rows // CZ, slots, 0)
    full = pay[...]
    hi = full.astype(BF16)
    hl[0 : pn.width, :] = hi
    hl[pn.width :, :] = (full - hi.astype(F32)).astype(BF16)

    mine = lax.div(me, pn.stride)
    owner = jnp.logical_and(lax.rem(me, pn.stride) == 0, mine < pn.tiles)

    @pl.when(owner)
    def _():
        grs[me] = gpart[tile(mine), :]
        others(lambda p: remote(gpart.at[tile(0), :], grs.at[p], rs_s.at[0], rs_r.at[p], p).wait_recv())
        total = jnp.sum(grs[...], axis=0)
        gsnd[...] = total
        gfull[mine] = total
        others(lambda p: remote(gsnd, gfull.at[mine], ag_s.at[p], ag_r.at[mine], p).start())

    lane = lax.broadcasted_iota(jnp.int32, (1, CZ), 1)
    block = lax.div(me, pn.per_blk)

    def spread(parts, q):
        out = None
        for j, value in enumerate(parts):
            amount = (j - q) * pn.cap % CZ
            moved = pltpu.roll(value, amount, 1) if amount else value
            out = moved if out is None else jnp.where(lane >= j * pn.cap, moved, out)
        return out

    def pack(it, _):
        gb = lax.rem(block + it, pn.nblk)
        for half in range(2):
            ids = lane + (gb * 256 + half * CZ)
            ohp[gb, :, half * CZ : (half + 1) * CZ] = jnp.where(slot[...] == ids, 1.0, 0.0).astype(BF16)
        oh = ohp[gb]
        xs[...] = jnp.dot(hl[0 : pn.width, :], oh, preferred_element_type=F32)
        xs[...] += jnp.dot(hl[pn.width :, :], oh, preferred_element_type=F32)
        for half in range(2):
            parts = [xs[j * pn.part : (j + 1) * pn.part, half * CZ : (half + 1) * CZ] for j in range(pn.fold)]
            for q in range(pn.fold):
                p = gb * pn.per_blk + half * pn.fold + q
                packet = spread(parts, q)

                @pl.when(p == me)
                def _():
                    got[p] = packet

                @pl.when(p != me)
                def _():
                    snd[p] = packet
                    remote(snd.at[p], got.at[me], bulk_s.at[p], bulk_r.at[me], p).start()
        return 0

    lax.fori_loop(0, pn.nblk, pack, 0)

    for y in range(CY):
        uv[pl.ds(y, pn.basis_rows, stride=CY), :] = u_ref[:, y * CZ : (y + 1) * CZ]
    mred[...] = jnp.zeros(mred.shape, F32)
    ginv[...] = jnp.zeros(ginv.shape, F32)

    def ag_wait(t, _):
        own = t * pn.stride

        @pl.when(me != own)
        def _():
            remote(gsnd, gfull.at[t], ag_s.at[0], ag_r.at[t], own).wait_recv()
        return 0

    lax.fori_loop(0, pn.tiles, ag_wait, 0)
    sums = gfull[...].reshape(pn.tiles * 8, CZ)
    gm[...] = sums[0:k]
    sub_k = lax.broadcasted_iota(jnp.int32, (k, 1), 0)

    def sweep(i, _):
        m = gm[...]
        row = gm[pl.ds(i, 1), :]
        at = lane == i
        col = jnp.sum(jnp.where(at, m, 0.0), axis=1, keepdims=True)
        pivot = jnp.sum(jnp.where(at, row, 0.0), axis=1, keepdims=True)
        scaled = jnp.where(at, 1.0, row) / pivot
        inner = jnp.where(at, 0.0, m) - col * scaled
        gm[...] = jnp.where(sub_k == i, scaled, inner)
        return 0

    lax.fori_loop(0, k, sweep, 0)
    ginv[0:k, :] = gm[...]

    def solve(p):
        return jnp.dot(p, ginv[...], precision=HIGH, preferred_element_type=F32)

    def bdot(p, z):
        return jnp.sum(jnp.where(lane < k, p * z, 0.0), axis=1, keepdims=True)

    s_row = jnp.broadcast_to(sums[k : k + 1, :], (8, CZ))
    bb_all = jnp.broadcast_to(sums[k + 1 : k + 2, 0:1], (8, 1))
    z0 = solve(s_row)
    beta = jnp.sqrt(bb_all - bdot(s_row, z0))

    acc[...] = jnp.zeros(acc.shape, F32)
    sub_r = lax.broadcasted_iota(jnp.int32, (rows, 1), 0).astype(F32) + 1.0

    def unpack(it, _):
        gb = lax.rem(block - it + pn.nblk, pn.nblk)
        for half in range(2):
            values = []
            for q in range(pn.fold):
                p = gb * pn.per_blk + half * pn.fold + q

                @pl.when(p != me)
                def _():
                    remote(snd.at[p], got.at[p], bulk_s.at[p], bulk_r.at[p], p).wait_recv()
            for q in range(pn.fold):
                values.append(got[gb * pn.per_blk + half * pn.fold + q])
            for j in range(pn.fold):
                xs[j * pn.part : (j + 1) * pn.part, half * CZ : (half + 1) * CZ] = spread(values, j)
            tags = xs[pn.tag : pn.tag + 1, half * CZ : (half + 1) * CZ]
            oht[gb, :, half * CZ : (half + 1) * CZ] = jnp.where(sub_r == tags, 1.0, 0.0).astype(BF16)
        x = xs[...]
        xh = x.astype(BF16)
        xhl[0 : pn.width, :] = xh
        xhl[pn.width :, :] = (x - xh.astype(F32)).astype(BF16)
        for n in range(rows // 256):
            at = slice(n * 256, (n + 1) * 256)
            o = oht[gb, at, :]
            acc[:, at] += lax.dot_general(xhl[0 : pn.width, :], o, NT, preferred_element_type=F32)
            acc[:, at] += lax.dot_general(xhl[pn.width :, :], o, NT, preferred_element_type=F32)
        return 0

    lax.fori_loop(0, pn.nblk, unpack, 0)
    for y in range(CY):
        new[pl.ds(y, pn.width, stride=CY), :] = acc[:, y * CZ : (y + 1) * CZ]

    def row(i):
        return new[i * CY : (i + 1) * CY, :]

    sub = lax.broadcasted_iota(jnp.int32, (CY, CZ), 0)
    lane8 = lax.broadcasted_iota(jnp.int32, (CY, CZ), 1)

    def combine(get, z):
        out = [jnp.zeros((CY, CZ), F32)] * 3
        for m in range(k):
            zb = jnp.broadcast_to(z[:, m : m + 1], (CY, CZ))
            for a in range(3):
                out[a] = out[a] + get(a * k + m) * zb
        return out

    def c_row(i):
        return row(pn.c0 + i)

    def u_row(i):
        return uv[i * CY : (i + 1) * CY, :]

    places = ((-1, 0), (1, 0), (0, 1), (-1, 1), (1, 1))

    def apply_op(phase, v):
        for b in range(3):
            hsnd[phase, b] = v[b]
        for j, (dx, oy) in enumerate(places):
            to = gx - dx
            target = to * pn.ny + (lax.rem(gy + oy, 2))

            @pl.when(jnp.logical_and(to >= 0, to < pn.nx))
            def _():
                remote(hsnd.at[phase], hrcv.at[phase, j], h_s.at[phase, j], h_r.at[phase, j], target).start()
        for j, (dx, oy) in enumerate(places):
            there = gx + dx
            source = there * pn.ny + (lax.rem(gy + oy, 2))
            valid = jnp.logical_and(there >= 0, there < pn.nx)

            @pl.when(valid)
            def _():
                remote(hsnd.at[phase], hrcv.at[phase, j], h_s.at[phase, j], h_r.at[phase, j], source).wait_recv()

            @pl.when(jnp.logical_not(valid))
            def _():
                hrcv[phase, j] = jnp.zeros((3, CY, CZ), F32)
        out = [jnp.zeros((CY, CZ), F32)] * 3
        for dx in (-1, 0, 1):
            for b in range(3):
                near = v[b] if dx == 0 else hrcv[phase, places.index((dx, 0)), b]
                side = hrcv[phase, places.index((dx, 1)), b]
                for dy in (-1, 0, 1):
                    if dy == 0:
                        moved = near
                    elif dy == -1:
                        edge = jnp.where(gy > 0, pltpu.roll(side, 1, 0), 0.0)
                        moved = jnp.where(sub == 0, edge, pltpu.roll(near, 1, 0))
                    else:
                        edge = jnp.where(gy == 0, pltpu.roll(side, CY - 1, 0), 0.0)
                        moved = jnp.where(sub == CY - 1, edge, pltpu.roll(near, CY - 1, 0))
                    for dz in (-1, 0, 1):
                        if dz == 0:
                            value = moved
                        elif dz == -1:
                            value = jnp.where(lane8 == 0, 0.0, pltpu.roll(moved, 1, 1))
                        else:
                            value = jnp.where(lane8 == CZ - 1, 0.0, pltpu.roll(moved, CZ - 1, 1))
                        kk = (dx + 1) * 9 + (dy + 1) * 3 + dz + 1
                        for a in range(3):
                            out[a] = out[a] + row((kk * 3 + a) * 3 + b) * value
        return out

    def put(i, value):
        mred[i : i + 1, :] = jnp.sum(value, axis=0, keepdims=True)

    def dot3(p, q):
        return p[0] * q[0] + p[1] * q[1] + p[2] * q[2]

    def sums_of(phase, image, vectors):
        for m in range(k):
            put(m, dot3([c_row(a * k + m) for a in range(3)], image))
        for i, vector in enumerate(vectors + [image]):
            put(k + i, dot3(vector, image))
        mine_row = lax.dot_general(jnp.ones((8, CZ), F32), mred[...], NT, precision=HIGH, preferred_element_type=F32)
        rsnd[phase] = mine_row
        rrcv[phase, me] = mine_row
        others(lambda p: remote(rsnd.at[phase], rrcv.at[phase, me], red_s.at[phase, p], red_r.at[phase, me], p).start())
        others(lambda p: remote(rsnd.at[phase], rrcv.at[phase, p], red_s.at[phase, p], red_r.at[phase, p], p).wait_recv())
        return jnp.sum(rrcv[phase], axis=0)

    load = [row(pn.b0 + a) for a in range(3)]
    part = combine(c_row, z0)
    v1 = [(load[a] - part[a]) / beta for a in range(3)]
    w = apply_op(0, v1)
    p1 = sums_of(0, w, [v1])
    z1 = solve(p1)
    h11, ww = p1[:, k : k + 1], p1[:, k + 1 : k + 2]
    h21 = jnp.sqrt(ww - bdot(p1, z1) - h11 * h11)
    part = combine(c_row, z1)
    v2 = [(w[a] - part[a] - h11 * v1[a]) / h21 for a in range(3)]
    w = apply_op(1, v2)
    p2 = sums_of(1, w, [v1, v2])
    z2 = solve(p2)
    h12, h22, ww = p2[:, k : k + 1], p2[:, k + 1 : k + 2], p2[:, k + 2 : k + 3]
    h32 = jnp.sqrt(ww - bdot(p2, z2) - h12 * h12 - h22 * h22)
    m11 = h11 * h11 + h21 * h21
    m12 = h11 * h12 + h21 * h22
    m22 = h12 * h12 + h22 * h22 + h32 * h32
    g_one, g_two = beta * h11, beta * h12
    determ = m11 * m22 - m12 * m12
    y_one = (m22 * g_one - m12 * g_two) / determ
    y_two = (m11 * g_two - m12 * g_one) / determ

    ut = combine(u_row, z0 - y_one * z1 - y_two * z2)
    for y in range(CY):
        tile_y = jnp.zeros((8, CZ), F32)
        for a in range(3):
            tile_y = jnp.where(sub == a, jnp.broadcast_to(ut[a][y : y + 1, :], (8, CZ)), tile_y)
        high = tile_y.astype(BF16).astype(F32)
        ulhs[0:8, y * CZ : (y + 1) * CZ] = high
        ulhs[8:16, y * CZ : (y + 1) * CZ] = tile_y - high
    ub = ulhs[...].astype(BF16)

    def upack(gb, _):
        d = jnp.dot(ub, ohp[gb], preferred_element_type=F32)
        d = d[0:8] + d[8:16]
        usnd[2 * gb] = d[:, :CZ]
        usnd[2 * gb + 1] = d[:, CZ:]
        return 0

    lax.fori_loop(0, pn.nblk, upack, 0)
    others(lambda p: remote(usnd.at[lax.div(p, pn.fold)], urcv.at[me], u_s.at[p], u_r.at[me], p).start())
    urcv[me] = usnd[lax.div(me, pn.fold)]
    others(lambda p: remote(usnd.at[0], urcv.at[p], u_s.at[p], u_r.at[p], p).wait_recv())
    place = lax.rem(me, pn.fold)

    def uunpack(gb, total):
        halves = []
        for half in range(2):
            out = None
            for q in range(pn.fold):
                tile_q = urcv[gb * pn.per_blk + half * pn.fold + q]
                if pn.fold > 1:
                    tile_q = pltpu.roll(tile_q, lax.rem((q - place) * pn.cap + CZ, CZ), 1)
                out = tile_q if out is None else jnp.where(lane >= q * pn.cap, tile_q, out)
            halves.append(out)
        x = jnp.concatenate(halves, axis=1)
        high = x.astype(BF16).astype(F32)
        x2 = jnp.concatenate([high, x - high], axis=0).astype(BF16)
        return total + lax.dot_general(x2, oht[gb], NT, preferred_element_type=F32)

    moved = lax.fori_loop(0, pn.nblk, uunpack, jnp.zeros((16, rows), F32))
    moved = moved[0:8] + moved[8:16]
    sol = []
    for a in range(3):
        value = jnp.zeros((CY, CZ), F32)
        for y in range(CY):
            line = jnp.broadcast_to(moved[a : a + 1, y * CZ : (y + 1) * CZ], (CY, CZ))
            value = jnp.where(sub == y, line, value)
        sol.append(value + y_one * v1[a] + y_two * v2[a])
        sol_ref[a] = sol[a]
    w = apply_op(2, sol)
    for a in range(3):
        res_ref[a] = row(pn.b0 + a) - w[a]

    def rs_done(t, _):
        own = t * pn.stride

        @pl.when(me != own)
        def _():
            remote(gpart.at[tile(t), :], grs.at[me], rs_s.at[t], rs_r.at[me], own).wait_send()
        return 0

    lax.fori_loop(0, pn.tiles, rs_done, 0)

    @pl.when(owner)
    def _():
        others(lambda p: remote(gsnd, gfull.at[mine], ag_s.at[p], ag_r.at[mine], p).wait_send())

    others(lambda p: remote(snd.at[p], got.at[me], bulk_s.at[p], bulk_r.at[me], p).wait_send())
    for phase in range(2):
        others(lambda p: remote(rsnd.at[phase], rrcv.at[phase, me], red_s.at[phase, p], red_r.at[phase, me], p).wait_send())
    others(lambda p: remote(usnd.at[lax.div(p, pn.fold)], urcv.at[me], u_s.at[p], u_r.at[me], p).wait_send())
    for phase in range(3):
        for j, (dx, oy) in enumerate(places):
            to = gx - dx
            target = to * pn.ny + (lax.rem(gy + oy, 2))

            @pl.when(jnp.logical_and(to >= 0, to < pn.nx))
            def _():
                remote(hsnd.at[phase], hrcv.at[phase, j], h_s.at[phase, j], h_r.at[phase, j], target).wait_send()


def body(nx, ny, operator, basis_u, basis_c, right_side, new_rows):
    rows = operator.shape[1]
    pn = Plan(nx, ny, rows, operator.shape[0], basis_u.shape[0])
    n = pn.peers
    vmem, dma = pltpu.VMEM, pltpu.SemaphoreType.DMA
    out = jax.ShapeDtypeStruct((3, CY, CZ), F32)
    whole = pl.BlockSpec(memory_space=pltpu.VMEM)
    sol, res = pl.pallas_call(
        functools.partial(kernel, pn),
        out_shape=(out, out),
        in_specs=[whole] * 6,
        out_specs=(whole, whole),
        scratch_shapes=[
            vmem((pn.width, rows), F32),
            vmem((2 * pn.width, rows), BF16),
            vmem((rows, CZ), jnp.int32),
            vmem((pn.nblk, rows, 256), BF16),
            vmem((pn.width, 256), F32),
            vmem((n, pn.part, CZ), F32),
            vmem((n, pn.part, CZ), F32),
            vmem((2 * pn.width, 256), BF16),
            vmem((pn.nblk, rows, 256), BF16),
            vmem((pn.width, rows), F32),
            vmem((pn.width * CY, CZ), F32),
            vmem((pn.basis_rows * CY, CZ), F32),
            vmem((pn.tiles * 8, CZ), F32),
            vmem((n, 8, CZ), F32),
            vmem((8, CZ), F32),
            vmem((pn.tiles, 8, CZ), F32),
            vmem((pn.k, CZ), F32),
            vmem((CZ, CZ), F32),
            vmem((3, 3, CY, CZ), F32),
            vmem((3, 5, 3, CY, CZ), F32),
            vmem((CZ, CZ), F32),
            vmem((2, 8, CZ), F32),
            vmem((2, n, 8, CZ), F32),
            vmem((16, rows), F32),
            vmem((2 * pn.nblk, 8, CZ), F32),
            vmem((n, 8, CZ), F32),
            dma((n,)), dma((n,)),
            dma((pn.tiles,)), dma((n,)),
            dma((n,)), dma((pn.tiles,)),
            dma((3, 5)), dma((3, 5)),
            dma((2, n)), dma((2, n)),
            dma((n,)), dma((n,)),
        ],
        compiler_params=pltpu.CompilerParams(
            collective_id=0, has_side_effects=True, vmem_limit_bytes=60 << 20
        ),
        name="solve",
    )(operator, basis_u, basis_c, right_side, new_rows.reshape(rows, 1), new_rows.reshape(1, rows))
    return sol.reshape(3, rows), res.reshape(3, rows)


def solution(mesh):
    split = P(None, ("gx", "gy"))
    return jax.shard_map(
        functools.partial(body, mesh.shape["gx"], mesh.shape["gy"]),
        mesh=mesh,
        in_specs=(split, split, split, split, P(("gx", "gy"))),
        out_specs=(split, split),
        check_vma=False,
    )
```

time: 619 us -> 139 us (0.22); the launches traced: 611 us -> 139 us
  local copies, waits for them, and re-layouts: 171 us -> 3.04 us
  Pallas kernels: 0 us -> 135 us
  other arithmetic: 126 us -> 0 us
  blocking collectives: 125 us -> 0 us
  waiting for transfers between devices: 115 us -> 0 us
  starting transfers between devices: 47 us -> 0 us
  matrix products: 14.6 us -> 0 us
  between operations: 12 us -> 0.64 us
    pallas_call x0 -> x1, Pallas kernels: none -> 135 us  [body(): pl.pallas_call(functools.partial(kernel, pn), out_shape=(out, out), in_sp...]
    psum x3 -> x0, blocking collectives: 125 us -> none  [the longest x2 86.2 us: sums_of(): return lax.psum(local, ('gx', 'gy'))]
    all_to_all x2 -> x0, waiting for transfers between devices: 115 us -> none  [the longest x1 115 us: body(): lax.all_to_all(buffer, ('gx', 'gy'), split_axis=1, concat_axis=1, tiled=T...]
    reduce_sum x77 -> x0, other arithmetic: 79.1 us -> none  [the longest x69 62.8 us: stencil(): total = total + jnp.sum(coef[k] * moved[None], axis=1)]
    slice x36 -> x0, local copies, waits for them, and re-layouts: 56.9 us -> none  [the longest x29 49.3 us: stencil(): total = total + jnp.sum(coef[k] * moved[None], axis=1)]
    reduce_sum x30 -> x0, local copies, waits for them, and re-layouts: 44.8 us -> none  [stencil(): total = total + jnp.sum(coef[k] * moved[None], axis=1)]
    ppermute x12 -> x0, starting transfers between devices: 33.8 us -> none  [the longest x6 25.9 us: with_halo(): lax.ppermute(tail, axis, [(i, (i + 1) % count) for i in range(ends)])]
    unnamed x73 -> x0, local copies, waits for them, and re-layouts: 27.6 us -> none
  transfers between devices with their start and end apart: 14 -> 0, of which waited for: 1 -> 0; matrix products, arithmetic and copies ran while one was open for 18% -> 0% of each run, Pallas kernels for 0% -> 0%
where the time goes in v1:
time: 139 us
  Pallas kernels  135 us (97%)
  local copies, waits for them, and re-layouts  3.04 us (2%)
    pallas_call x1, Pallas kernels, body(): pl.pallas_call(functools.partial(kernel, pn), out_shape=(out, out), in_sp...  135 us

profile of v1, /device:TPU:0, one launch (start us, length us, event | category | flops | bytes accessed | tf_op | source)
XLA Modules:
  0.0 139.0 jit_solution(4415968322006779864)
XLA Ops:
  0.6 1.7 %copy.7.rcol_ref = s32[1024,1]{1,0:T(8,128)} copy(s32[1024,1]{0,1:T(1,128)} %bitcast.8) | data formatting | bytes 8192 | tf_op jit(solution)/shard_map/reshape | solution.py:495
  2.3 135.3 %solve.1 = (f32[3,8,128]{2,1,0:T(8,128)}, f32[3,8,128]{2,1,0:T(8,128)}) custom-call(f32[243,1024]{1,0:T(8,128)} %op_ref.1, f32[144,1024]{1,0:T(8,128)} %u_ref.1, f32[144,1024]{1,0:T(8,128)} %c_ref.1, f32[3,1024]{1,0:T(4,128)} %b_ref.1, s32[1024,1]{1,0:T(8,128)} %copy.7.rcol_ref, s32[1,1024]{1,0:T(1,128)} %bitcast.9), custom_call_target="tpu_custom_call" | custom-call | tf_op jit(solution)/shard_map/solve/pallas_call | solution.py:452
  137.6 1.3 copy_bitcast_fusion

commit v2 on v1

--- a/solution.py
+++ b/solution.py
@@ -40,10 +40,10 @@
 
 
 def kernel(
-    pn, op_ref, u_ref, c_ref, b_ref, rcol_ref, rrow_ref, sol_ref, res_ref,
+    pn, op_ref, u_ref, c_ref, b_ref, rrow_ref, sol_ref, res_ref,
     pay, hl, slot, ohp, xs, snd, got, xhl, oht, acc, new, uv,
     gpart, grs, gsnd, gfull, gm, ginv,
-    hsnd, hrcv, mred, rsnd, rrcv, ulhs, usnd, urcv,
+    hsnd, hrcv, mred, rsnd, rrcv, ulhs, usnd, urcv, utmp,
     bulk_s, bulk_r, rs_s, rs_r, ag_s, ag_r, h_s, h_r, red_s, red_r, u_s, u_r,
 ):
     gx, gy = lax.axis_index("gx"), lax.axis_index("gy")
@@ -111,9 +111,14 @@
     jrow = lax.broadcasted_iota(jnp.int32, (CZ, rows), 1)
     irow = lax.broadcasted_iota(jnp.int32, (CZ, rows), 0)
 
+    diagonal = (
+        lax.broadcasted_iota(jnp.int32, (CZ, CZ), 0) == lax.broadcasted_iota(jnp.int32, (CZ, CZ), 1)
+    )
+
     def slots(i, _):
         at = pl.ds(pl.multiple_of(i * CZ, CZ), CZ)
-        tc = lax.shift_right_logical(rcol_ref[at, :], shift)
+        line = lax.shift_right_logical(rrow_ref[:, at], shift).astype(F32)
+        tc = jnp.sum(jnp.where(diagonal, line, 0.0), axis=1, keepdims=True).astype(jnp.int32)
         before = jnp.logical_and(tc == trow, jrow < irow + i * CZ)
         rank = jnp.sum(jnp.where(before, 1.0, 0.0), axis=1, keepdims=True)
         slot[at, :] = jnp.broadcast_to(tc * pn.cap + rank.astype(jnp.int32), (CZ, CZ))
@@ -124,18 +129,6 @@
     hi = full.astype(BF16)
     hl[0 : pn.width, :] = hi
     hl[pn.width :, :] = (full - hi.astype(F32)).astype(BF16)
-
-    mine = lax.div(me, pn.stride)
-    owner = jnp.logical_and(lax.rem(me, pn.stride) == 0, mine < pn.tiles)
-
-    @pl.when(owner)
-    def _():
-        grs[me] = gpart[tile(mine), :]
-        others(lambda p: remote(gpart.at[tile(0), :], grs.at[p], rs_s.at[0], rs_r.at[p], p).wait_recv())
-        total = jnp.sum(grs[...], axis=0)
-        gsnd[...] = total
-        gfull[mine] = total
-        others(lambda p: remote(gsnd, gfull.at[mine], ag_s.at[p], ag_r.at[mine], p).start())
 
     lane = lax.broadcasted_iota(jnp.int32, (1, CZ), 1)
     block = lax.div(me, pn.per_blk)
@@ -172,7 +165,21 @@
                     remote(snd.at[p], got.at[me], bulk_s.at[p], bulk_r.at[me], p).start()
         return 0
 
-    lax.fori_loop(0, pn.nblk, pack, 0)
+    lax.fori_loop(0, 2, pack, 0)
+
+    mine = lax.div(me, pn.stride)
+    owner = jnp.logical_and(lax.rem(me, pn.stride) == 0, mine < pn.tiles)
+
+    @pl.when(owner)
+    def _():
+        grs[me] = gpart[tile(mine), :]
+        others(lambda p: remote(gpart.at[tile(0), :], grs.at[p], rs_s.at[0], rs_r.at[p], p).wait_recv())
+        total = jnp.sum(grs[...], axis=0)
+        gsnd[...] = total
+        gfull[mine] = total
+        others(lambda p: remote(gsnd, gfull.at[mine], ag_s.at[p], ag_r.at[mine], p).start())
+
+    lax.fori_loop(2, pn.nblk, pack, 0)
 
     for y in range(CY):
         uv[pl.ds(y, pn.basis_rows, stride=CY), :] = u_ref[:, y * CZ : (y + 1) * CZ]
@@ -220,8 +227,13 @@
     acc[...] = jnp.zeros(acc.shape, F32)
     sub_r = lax.broadcasted_iota(jnp.int32, (rows, 1), 0).astype(F32) + 1.0
 
+    half_n = pn.nblk // 2
+
     def unpack(it, _):
-        gb = lax.rem(block - it + pn.nblk, pn.nblk)
+        far = lax.div(it, half_n)
+        side = lax.rem(lax.div(block, half_n) + far, 2)
+        start = jnp.where(far == 0, block, half_n - 1)
+        gb = side * half_n + lax.rem(start - it + 2 * pn.nblk, half_n)
         for half in range(2):
             values = []
             for q in range(pn.fold):
@@ -248,8 +260,12 @@
         return 0
 
     lax.fori_loop(0, pn.nblk, unpack, 0)
-    for y in range(CY):
-        new[pl.ds(y, pn.width, stride=CY), :] = acc[:, y * CZ : (y + 1) * CZ]
+
+    def relayout(first, last):
+        for y in range(CY):
+            new[pl.ds(first * CY + y, last - first, stride=CY), :] = acc[first:last, y * CZ : (y + 1) * CZ]
+
+    relayout(pn.c0, pn.width)
 
     def row(i):
         return new[i * CY : (i + 1) * CY, :]
@@ -273,7 +289,7 @@
 
     places = ((-1, 0), (1, 0), (0, 1), (-1, 1), (1, 1))
 
-    def apply_op(phase, v):
+    def apply_op(phase, v, between=None):
         for b in range(3):
             hsnd[phase, b] = v[b]
         for j, (dx, oy) in enumerate(places):
@@ -283,6 +299,8 @@
             @pl.when(jnp.logical_and(to >= 0, to < pn.nx))
             def _():
                 remote(hsnd.at[phase], hrcv.at[phase, j], h_s.at[phase, j], h_r.at[phase, j], target).start()
+        if between is not None:
+            between()
         for j, (dx, oy) in enumerate(places):
             there = gx + dx
             source = there * pn.ny + (lax.rem(gy + oy, 2))
@@ -332,17 +350,17 @@
             put(m, dot3([c_row(a * k + m) for a in range(3)], image))
         for i, vector in enumerate(vectors + [image]):
             put(k + i, dot3(vector, image))
-        mine_row = lax.dot_general(jnp.ones((8, CZ), F32), mred[...], NT, precision=HIGH, preferred_element_type=F32)
+        mine_row = lax.dot_general(jnp.ones((8, CZ), F32), mred[...], NT, precision=HIGH, preferred_element_type=F32)[0:1]
         rsnd[phase] = mine_row
         rrcv[phase, me] = mine_row
         others(lambda p: remote(rsnd.at[phase], rrcv.at[phase, me], red_s.at[phase, p], red_r.at[phase, me], p).start())
         others(lambda p: remote(rsnd.at[phase], rrcv.at[phase, p], red_s.at[phase, p], red_r.at[phase, p], p).wait_recv())
-        return jnp.sum(rrcv[phase], axis=0)
+        return jnp.broadcast_to(jnp.sum(rrcv[phase], axis=0), (8, CZ))
 
     load = [row(pn.b0 + a) for a in range(3)]
     part = combine(c_row, z0)
     v1 = [(load[a] - part[a]) / beta for a in range(3)]
-    w = apply_op(0, v1)
+    w = apply_op(0, v1, lambda: relayout(0, pn.c0))
     p1 = sums_of(0, w, [v1])
     z1 = solve(p1)
     h11, ww = p1[:, k : k + 1], p1[:, k + 1 : k + 2]
@@ -375,8 +393,8 @@
     def upack(gb, _):
         d = jnp.dot(ub, ohp[gb], preferred_element_type=F32)
         d = d[0:8] + d[8:16]
-        usnd[2 * gb] = d[:, :CZ]
-        usnd[2 * gb + 1] = d[:, CZ:]
+        usnd[2 * gb] = d[0:4, :CZ]
+        usnd[2 * gb + 1] = d[0:4, CZ:]
         return 0
 
     lax.fori_loop(0, pn.nblk, upack, 0)
@@ -384,13 +402,16 @@
     urcv[me] = usnd[lax.div(me, pn.fold)]
     others(lambda p: remote(usnd.at[0], urcv.at[p], u_s.at[p], u_r.at[p], p).wait_recv())
     place = lax.rem(me, pn.fold)
+    utmp[...] = jnp.zeros(utmp.shape, F32)
 
     def uunpack(gb, total):
         halves = []
         for half in range(2):
             out = None
             for q in range(pn.fold):
-                tile_q = urcv[gb * pn.per_blk + half * pn.fold + q]
+                at = (half * pn.fold + q) * 8
+                utmp[at : at + 4, :] = urcv[gb * pn.per_blk + half * pn.fold + q]
+                tile_q = utmp[at : at + 8, :]
                 if pn.fold > 1:
                     tile_q = pltpu.roll(tile_q, lax.rem((q - place) * pn.cap + CZ, CZ), 1)
                 out = tile_q if out is None else jnp.where(lane >= q * pn.cap, tile_q, out)
@@ -452,7 +473,7 @@
     sol, res = pl.pallas_call(
         functools.partial(kernel, pn),
         out_shape=(out, out),
-        in_specs=[whole] * 6,
+        in_specs=[whole] * 5,
         out_specs=(whole, whole),
         scratch_shapes=[
             vmem((pn.width, rows), F32),
@@ -476,11 +497,12 @@
             vmem((3, 3, CY, CZ), F32),
             vmem((3, 5, 3, CY, CZ), F32),
             vmem((CZ, CZ), F32),
-            vmem((2, 8, CZ), F32),
-            vmem((2, n, 8, CZ), F32),
+            vmem((2, 1, CZ), F32),
+            vmem((2, n, 1, CZ), F32),
             vmem((16, rows), F32),
-            vmem((2 * pn.nblk, 8, CZ), F32),
-            vmem((n, 8, CZ), F32),
+            vmem((2 * pn.nblk, 4, CZ), F32),
+            vmem((n, 4, CZ), F32),
+            vmem((pn.per_blk * 8, CZ), F32),
             dma((n,)), dma((n,)),
             dma((pn.tiles,)), dma((n,)),
             dma((n,)), dma((pn.tiles,)),
@@ -492,7 +514,7 @@
             collective_id=0, has_side_effects=True, vmem_limit_bytes=60 << 20
         ),
         name="solve",
-    )(operator, basis_u, basis_c, right_side, new_rows.reshape(rows, 1), new_rows.reshape(1, rows))
+    )(operator, basis_u, basis_c, right_side, new_rows.reshape(1, rows))
     return sol.reshape(3, rows), res.reshape(3, rows)
 
 

time: 139 us -> 133 us (0.957)
  Pallas kernels: 135 us -> 130 us
  local copies, waits for them, and re-layouts: 3.04 us -> 1.34 us
    pallas_call x1, Pallas kernels: 135 us -> 130 us  [body(): pl.pallas_call(functools.partial(kernel, pn), out_shape=(out, out), in_sp...]
    reshape x1 -> x0, local copies, waits for them, and re-layouts: 1.69 us -> none  [body(): new_rows.reshape(rows, 1)]
where the time goes in v2:
time: 133 us; the launch traced here: 132 us
  Pallas kernels  130 us (98%)
  local copies, waits for them, and re-layouts  1.34 us (1%)
    pallas_call x1, Pallas kernels, body(): pl.pallas_call(functools.partial(kernel, pn), out_shape=(out, out), in_sp...  130 us

profile of v2, /device:TPU:0, one launch (start us, length us, event | category | flops | bytes accessed | tf_op | source)
XLA Modules:
  0.0 132.5 jit_solution(3980210188096981599)
XLA Ops:
  0.6 130.5 %solve.1 = (f32[3,8,128]{2,1,0:T(8,128)}, f32[3,8,128]{2,1,0:T(8,128)}) custom-call(f32[243,1024]{1,0:T(8,128)} %op_ref.1, f32[144,1024]{1,0:T(8,128)} %u_ref.1, f32[144,1024]{1,0:T(8,128)} %c_ref.1, f32[3,1024]{1,0:T(4,128)} %b_ref.1, s32[1,1024]{1,0:T(1,128)} %bitcast.9), custom_call_target="tpu_custom_call" | custom-call | tf_op jit(solution)/shard_map/solve/pallas_call | solution.py:473
  131.1 1.3 %copy_bitcast_fusion = (f32[3,1024]{1,0:T(4,128)}, f32[3,1024]{1,0:T(4,128)}) fusion(f32[1,3,8,128]{3,2,1,0:T(8,128)} %bitcast.8, f32[1,3,8,128]{3,2,1,0:T(8,128)} %bitcast.7), kind=kLoop, calls=%fused_computation | loop fusion | bytes 49152 | tf_op jit(solution)/shard_map/reshape | solution.py:518
